TPU v7x, 128 devices: a whole 4x4x4 slice. The times are simulated.
128 devices in a mesh: fsdp: 32 (over z, x_hi, y), tp: 4 (over x_lo, core).
Axes of the slice: x: 4 (x_hi: 2, x_lo: 2; x = x_hi * 2 + x_lo), y: 4, z: 4, core: 2. Of those that a mesh axis runs over, the one named last changes fastest.
Arguments:
- base_o: bfloat16 [2, 8192, 8192], P(None, 'tp', 'fsdp'), may hold values from -0.0625 to 0.0625
- base_down: bfloat16 [2, 28672, 8192], P(None, 'tp', 'fsdp'), may hold values from -0.03125 to 0.03125
- factor_a_o: bfloat16 [2, 64, 4, 2048], P(None, None, None, 'fsdp'), may hold values from -0.0625 to 0.0625
- factor_b_o: bfloat16 [2, 8192, 64], P(None, 'fsdp'), may hold values from -1.1953125 to 1.1953125
- factor_a_down: bfloat16 [2, 64, 4, 7168], P(None, None, None, 'fsdp'), may hold values from -0.03125 to 0.03125
- factor_b_down: bfloat16 [2, 8192, 64], P(None, 'fsdp'), may hold values from -1.1953125 to 1.1953125
- magnitude_o: float32 [2, 8192], P(None, 'fsdp'), may hold values from 30 to 300
- magnitude_down: float32 [2, 8192], P(None, 'fsdp'), may hold values from 30 to 300
Outputs:
- merged_o: bfloat16 [2, 8192, 8192], P(None, 'tp', 'fsdp')
- merged_down: bfloat16 [2, 28672, 8192], P(None, 'tp', 'fsdp')
All inputs are finite; a program needn't handle non-finite values.
Results may differ from a plain program's by a relative error of at most 0.001.
Values may be sent and summed in bfloat16 or wider, within the bound.
No kernel may reach another device: no remote copies, remote signals or barrier semaphores. Data moves between devices by JAX's collectives and lax.ppermute only.
A program may use at most 128 MiB of HBM per device.

v0:
```python
import jax
import jax.numpy as jnp
from jax import lax
from jax.sharding import Mesh
from jax.sharding import PartitionSpec as P

TP = ("tp_0", "tp_1")


def copy_for_each(shard, axis):
    devices = lax.axis_size(axis)
    return lax.all_to_all(
        jnp.broadcast_to(shard[None], (devices, *shard.shape)), axis, 0, 0, tiled=True
    )


def joined_along(tiles, dim):
    tiles = jnp.moveaxis(tiles, 0, dim)
    lengths = tiles.shape
    return tiles.reshape(*lengths[:dim], lengths[dim] * lengths[dim + 1], *lengths[dim + 2 :])


def gather_directly(shard, axis, dim):
    tiles = copy_for_each(shard, axis)
    return joined_along(tiles, dim)


def one_axis_at_a_time(shard, axes):
    for axis in axes:
        shard = lax.psum(shard, axis)
    return shard


def of_everyone(shard, axis):
    everything = copy_for_each(shard, axis)
    return jnp.sum(everything, axis=0)


def low_rank(rows_a, factor_b):
    return jnp.einsum("lri,lor->lio", rows_a, factor_b, preferred_element_type=jnp.float32)


def squares(base, delta):
    summed = base.astype(jnp.float32) + 0.25 * delta
    return (summed, jnp.sum(summed * summed, axis=1))


def finish(summed, square, magnitude):
    return (magnitude[:, None, :] * summed * lax.rsqrt(square + 1e-06)[:, None, :]).astype(
        jnp.bfloat16
    )


def local(
    base_o,
    base_down,
    factor_a_o,
    factor_b_o,
    factor_a_down,
    factor_b_down,
    magnitude_o,
    magnitude_down,
):
    column_t = lax.axis_index(TP)
    own_o = lax.dynamic_index_in_dim(factor_a_o, column_t, 2, keepdims=False)
    delta_o = low_rank(gather_directly(own_o, "fsdp", 2), factor_b_o)
    own_down = lax.dynamic_index_in_dim(factor_a_down, column_t, 2, keepdims=False)
    delta_down = low_rank(gather_directly(own_down, "fsdp", 2), factor_b_down)
    summed_o, partial_o = squares(base_o, delta_o)
    square_o = one_axis_at_a_time(partial_o, TP)
    merged_o = finish(summed_o, square_o, magnitude_o)
    summed_down, partial_down = squares(base_down, delta_down)
    square_down = of_everyone(partial_down, TP)
    merged_down = finish(summed_down, square_down, magnitude_down)
    return (merged_o, merged_down)


def solution(mesh):
    finer = Mesh(mesh.devices.reshape(mesh.shape["fsdp"], 2, 2), ("fsdp", "tp_0", "tp_1"))
    in_specs = (
        P(None, TP, "fsdp"),
        P(None, TP, "fsdp"),
        P(None, None, None, "fsdp"),
        P(None, "fsdp", None),
        P(None, None, None, "fsdp"),
        P(None, "fsdp", None),
        P(None, "fsdp"),
        P(None, "fsdp"),
    )
    out_specs = (P(None, TP, "fsdp"), P(None, TP, "fsdp"))
    return jax.shard_map(local, mesh=finer, in_specs=in_specs, out_specs=out_specs, check_vma=False)
```

profile of v0, /device:TPU:1, one launch (start us, length us, event | category | flops | bytes accessed | tf_op | source)
XLA Modules:
  0.0 97.1 jit_solution(17505363252157816770)
XLA Ops:
  0.6 0.0 copy-start
  0.7 1.0 %constant_dynamic-slice_fusion.1 = bf16[2,64,1,64]{3,2,1,0:T(2,128)(2,1)S(1)} fusion(bf16[2,64,4,64]{3,2,1,0:T(4,128)(2,1)} %param.10, s32[]{:T(128)S(6)} %select_n.6), kind=kLoop, calls=%fused_computation.11 | loop fusion | bytes 32772 | tf_op jit(solution)/shard_map/jit(dynamic_index_in_dim)/dynamic_slice | solution.py:65
  1.7 0.2 broadcast_in_dim.11
  1.9 1.5 %reshape.24 = bf16[32,2,4096]{2,1,0:T(2,128)(2,1)} reshape(bf16[32,2,64,64]{3,2,1,0:T(8,128)(2,1)S(1)} %broadcast_in_dim.11) | data formatting | bytes 1048576
  3.5 11.3 %all-to-all-start = ((bf16[32,2,4096]{2,1,0:T(2,128)(2,1)}), bf16[32,2,4096]{2,1,0:T(2,128)(2,1)S(1)}, u32[]{:S(2)}, u32[]{:S(2)}) async-start(bf16[32,2,4096]{2,1,0:T(2,128)(2,1)} %reshape.24), calls=%async_computation | async-start | bytes 1048576 | tf_op jit(solution)/shard_map/all_to_all | solution.py:12
  14.8 0.0 copy-done
  14.8 0.1 constant_dynamic-slice_fusion
  15.0 11.2 %all-to-all-done = bf16[32,2,4096]{2,1,0:T(2,128)(2,1)S(1)} async-done(((bf16[32,2,4096]{2,1,0:T(2,128)(2,1)}), bf16[32,2,4096]{2,1,0:T(2,128)(2,1)S(1)}, u32[]{:S(2)}, u32[]{:S(2)}) %all-to-all-start) | async-done | bytes 524320 | tf_op jit(solution)/shard_map/all_to_all | solution.py:12
  26.2 0.0 copy-start.1
  26.2 1.6 %broadcast_in_dim.13 = bf16[32,2,64,224]{3,2,1,0:T(8,128)(2,1)} broadcast(bf16[2,64,224]{2,1,0:T(8,128)(2,1)S(1)} %bitcast.18), dimensions={1,2,3} | broadcast | bytes 1892352 | tf_op jit(solution)/shard_map/broadcast_in_dim | solution.py:13
  27.8 0.0 copy-start.2
  27.8 0.0 copy-done.1
  27.8 6.0 %all-to-all-start.1 = ((bf16[32,2,64,224]{3,2,1,0:T(8,128)(2,1)}), bf16[32,2,64,224]{3,2,1,0:T(8,128)(2,1)S(1)}, u32[]{:S(2)}, u32[]{:S(2)}) async-start(bf16[32,2,64,224]{3,2,1,0:T(8,128)(2,1)} %broadcast_in_dim.13), calls=%async_computation.1 | async-start | bytes 4194304 | tf_op jit(solution)/shard_map/all_to_all | solution.py:12
  33.8 2.3 %reshape.25 = bf16[32,2,64,64]{3,2,1,0:T(8,128)(2,1)S(1)} reshape(bf16[32,2,4096]{2,1,0:T(2,128)(2,1)} %copy-done.1) | data formatting | bytes 1048576
  36.1 1.6 %copy.21 = bf16[2,64,32,64]{3,2,1,0:T(8,128)(2,1)} copy(bf16[2,64,32,64]{3,1,0,2:T(8,128)(2,1)S(1)} %bitcast.17) | data formatting | bytes 1048576 | tf_op jit(solution)/shard_map/transpose | solution.py:18
  37.8 2.0 %reshape.22 = bf16[2,64,2048]{2,1,0:T(8,128)(2,1)S(1)} reshape(bf16[2,64,32,64]{3,2,1,0:T(8,128)(2,1)} %copy.21) | data formatting | bytes 1048576 | tf_op jit(solution)/shard_map/reshape | solution.py:20
  39.8 0.0 copy-done.2
  39.8 4.6 %multiply_reduce_fusion.1 = (f32[2,256]{1,0:T(2,128)S(1)}, f32[2,2048,256]{2,1,0:T(8,128)}) fusion(bf16[2,64,2048]{2,1,0:T(8,128)(2,1)S(1)} %reshape.22, bf16[2,256,64]{1,2,0:T(8,128)(2,1)S(1)} %copy-done.2, bf16[2,2048,256]{2,1,0:T(8,128)(2,1)} %param.8), kind=kOutput, calls=%fused_computation.4 | convolution fusion | flops 139460096 | bytes 6883328 | tf_op jit(solution)/shard_map/lri,lor->lio/dot_general | solution.py:40
  44.4 0.0 copy-start.3
  44.4 13.0 %psum.14 = f32[2,256]{1,0:T(2,128)S(1)} all-reduce(f32[2,256]{1,0:T(2,128)S(1)} %get-tuple-element.2), channel_id=1, replica_groups=mesh['fsdp'=32,'tp_0'=2,'tp_1'=2] {'tp_0'}, use_global_device_ids=true, to_apply=%region_1.2 | all-reduce | flops 512 | bytes 4096 | tf_op jit(solution)/shard_map/psum | solution.py:30
  57.5 3.9 %psum.15 = f32[2,256]{1,0:T(2,128)S(1)} all-reduce(f32[2,256]{1,0:T(2,128)S(1)} %psum.14), channel_id=1, replica_groups=mesh['fsdp'=32,'tp_0'=2,'tp_1'=2] {'tp_1'}, use_global_device_ids=true, to_apply=%region_2.3 | all-reduce | flops 512 | bytes 4096 | tf_op jit(solution)/shard_map/psum | solution.py:30
  61.4 0.5 all-to-all-done.1
  61.8 2.5 %copy.23 = bf16[2,64,32,224]{3,2,1,0:T(8,128)(2,1)} copy(bf16[2,64,32,224]{3,1,0,2:T(8,128)(2,1)S(1)} %bitcast.16) | data formatting | bytes 3670016 | tf_op jit(solution)/shard_map/transpose | solution.py:18
  64.3 4.3 %reshape.23 = bf16[2,64,7168]{2,1,0:T(8,128)(2,1)S(1)} reshape(bf16[2,64,32,224]{3,2,1,0:T(8,128)(2,1)} %copy.23) | data formatting | bytes 3670016 | tf_op jit(solution)/shard_map/reshape | solution.py:20
  68.7 0.0 copy-done.3
  68.7 0.0 copy-start.4
  68.7 9.0 %multiply_reduce_fusion = (f32[2,256]{1,0:T(2,128)S(1)}, f32[2,7168,256]{2,1,0:T(8,128)}) fusion(bf16[2,64,7168]{2,1,0:T(8,128)(2,1)S(1)} %reshape.23, bf16[2,256,64]{1,2,0:T(8,128)(2,1)S(1)} %copy-done.3, bf16[2,7168,256]{2,1,0:T(8,128)(2,1)} %param.9), kind=kOutput, calls=%fused_computation.1 | convolution fusion | flops 488111616 | bytes 23922688 | tf_op jit(solution)/shard_map/lri,lor->lio/dot_general | solution.py:40
  77.7 0.0 copy-start.5
  77.7 0.6 broadcast_in_dim.14
  78.3 5.3 %all-to-all-start.2 = ((f32[4,2,256]{2,1,0:T(2,128)}), f32[4,2,256]{2,1,0:T(2,128)S(1)}, u32[]{:S(2)}, u32[]{:S(2)}) async-start(f32[4,2,256]{2,1,0:T(2,128)} %broadcast_in_dim.14), calls=%async_computation.2 | async-start | bytes 16384 | tf_op jit(solution)/shard_map/all_to_all | solution.py:12
  83.5 0.0 copy-done.4
  83.5 3.9 %multiply_convert_fusion.1 = bf16[2,2048,256]{2,1,0:T(8,128)(2,1)} fusion(f32[2,2048,256]{2,1,0:T(8,128)} %get-tuple-element.3, f32[2,256]{1,0:T(2,128)S(1)} %add_rsqrt_fusion.1, f32[2,256]{1,0:T(2,128)S(1)} %copy-done.4), kind=kLoop, calls=%fused_computation.3 | loop fusion | flops 3145728 | bytes 6295552 | tf_op jit(solution)/shard_map/convert_element_type | solution.py:49
  87.4 0.0 all-to-all-done.2
  87.5 0.0 copy-done.5
  87.5 9.6 %multiply_convert_fusion = bf16[2,7168,256]{2,1,0:T(8,128)(2,1)} fusion(f32[2,7168,256]{2,1,0:T(8,128)} %get-tuple-element.5, f32[2,256]{1,0:T(2,128)S(1)} %add_rsqrt_fusion, f32[2,256]{1,0:T(2,128)S(1)} %copy-done.5), kind=kLoop, calls=%fused_computation | loop fusion | flops 11010048 | bytes 22024192 | tf_op jit(solution)/shard_map/convert_element_type | solution.py:49
  (5 shorter events, 0.0 us)
Async XLA Ops:
  0.6 14.2 %copy-start = (bf16[2,64,4,224]{3,2,1,0:T(4,128)(2,1)S(1)}, bf16[2,64,4,224]{3,2,1,0:T(4,128)(2,1)}, u32[]{:S(2)}) copy-start(bf16[2,64,4,224]{3,2,1,0:T(4,128)(2,1)} %param.12) | copy-start | bytes 688132
  3.5 22.7 %all-to-all-start = ((bf16[32,2,4096]{2,1,0:T(2,128)(2,1)}), bf16[32,2,4096]{2,1,0:T(2,128)(2,1)S(1)}, u32[]{:S(2)}, u32[]{:S(2)}) async-start(bf16[32,2,4096]{2,1,0:T(2,128)(2,1)} %reshape.24), calls=%async_computation | async-start | bytes 1048576 | tf_op jit(solution)/shard_map/all_to_all | solution.py:12
  26.2 1.6 %copy-start.1 = (bf16[32,2,4096]{2,1,0:T(2,128)(2,1)}, bf16[32,2,4096]{2,1,0:T(2,128)(2,1)S(1)}, u32[]{:S(2)}) copy-start(bf16[32,2,4096]{2,1,0:T(2,128)(2,1)S(1)} %all-to-all-done) | copy-start | bytes 1572868
  27.8 12.1 %copy-start.2 = (bf16[2,256,64]{1,2,0:T(8,128)(2,1)S(1)}, bf16[2,256,64]{1,2,0:T(8,128)(2,1)}, u32[]{:S(2)}) copy-start(bf16[2,256,64]{1,2,0:T(8,128)(2,1)} %param.11) | copy-start | bytes 196612
  27.8 34.1 %all-to-all-start.1 = ((bf16[32,2,64,224]{3,2,1,0:T(8,128)(2,1)}), bf16[32,2,64,224]{3,2,1,0:T(8,128)(2,1)S(1)}, u32[]{:S(2)}, u32[]{:S(2)}) async-start(bf16[32,2,64,224]{3,2,1,0:T(8,128)(2,1)} %broadcast_in_dim.13), calls=%async_computation.1 | async-start | bytes 4194304 | tf_op jit(solution)/shard_map/all_to_all | solution.py:12
  44.4 24.2 %copy-start.3 = (bf16[2,256,64]{1,2,0:T(8,128)(2,1)S(1)}, bf16[2,256,64]{1,2,0:T(8,128)(2,1)}, u32[]{:S(2)}) copy-start(bf16[2,256,64]{1,2,0:T(8,128)(2,1)} %param.13) | copy-start | bytes 196612
  68.7 14.9 %copy-start.4 = (f32[2,256]{1,0:T(2,128)S(1)}, f32[2,256]{1,0:T(2,128)}, u32[]{:S(2)}) copy-start(f32[2,256]{1,0:T(2,128)} %param.14) | copy-start | bytes 6148
  77.7 9.8 %copy-start.5 = (f32[2,256]{1,0:T(2,128)S(1)}, f32[2,256]{1,0:T(2,128)}, u32[]{:S(2)}) copy-start(f32[2,256]{1,0:T(2,128)} %param.15) | copy-start | bytes 6148
  78.3 9.2 %all-to-all-start.2 = ((f32[4,2,256]{2,1,0:T(2,128)}), f32[4,2,256]{2,1,0:T(2,128)S(1)}, u32[]{:S(2)}, u32[]{:S(2)}) async-start(f32[4,2,256]{2,1,0:T(2,128)} %broadcast_in_dim.14), calls=%async_computation.2 | async-start | bytes 16384 | tf_op jit(solution)/shard_map/all_to_all | solution.py:12
where the time goes:
time: 97.7 us; the launch traced here: 97.1 us
  starting transfers between devices  22.6 us (23%)
  local copies, waits for them, and re-layouts  18 us (18%)
  blocking collectives  16.9 us (17%)
  matrix products  13.6 us (14%)
  other arithmetic  13.5 us (14%)
  waiting for transfers between devices  11.6 us (12%)
    all_to_all x3, starting transfers between devices, copy_for_each(): lax.all_to_all(jnp.broadcast_to(shard[None], (devices, *shard.shape)), ax...  22.6 us
    psum x2, blocking collectives, one_axis_at_a_time(): shard = lax.psum(shard, axis)  16.9 us
    dot_general x2, matrix products, low_rank(): jnp.einsum('lri,lor->lio', rows_a, factor_b, preferred_element_type=jnp.f...  13.6 us
    convert_element_type x2, other arithmetic, finish(): (magnitude[:, None, :] * summed * lax.rsqrt(square + 1e-06)[:, None, :])....  13.5 us
    all_to_all x3, waiting for transfers between devices, copy_for_each(): lax.all_to_all(jnp.broadcast_to(shard[None], (devices, *shard.shape)), ax...  11.6 us
    reshape x2, local copies, waits for them, and re-layouts, joined_along(): tiles.reshape(*lengths[:dim], lengths[dim] * lengths[dim + 1], *lengths[d...  6.37 us
    transpose x2, local copies, waits for them, and re-layouts, joined_along(): tiles = jnp.moveaxis(tiles, 0, dim)  4.15 us
    unnamed x16, local copies, waits for them, and re-layouts  3.88 us
  transfers between devices with their start and end apart: 3, of which 2 were waited for; matrix products, arithmetic and copies ran while one was open for 15% of the time, Pallas kernels for 0%

commit v1 on v0

v1 whole, which is shorter than its diff:
```python
import functools

import jax
import jax.numpy as jnp
import numpy as np
from jax import lax
from jax.experimental import pallas as pl
from jax.experimental.pallas import tpu as pltpu
from jax.sharding import Mesh
from jax.sharding import PartitionSpec as P

AXES = ("z", "xh", "y", "xl", "c")
SHAPE = (4, 2, 4, 2, 2)
TP = ("xl", "c")
FSDP = ("z", "xh", "y")
STEPS = (0, -1, 1, 2)
HALF = 144
DOWN = 224
ATTN = 64
TAIL = DOWN - HALF
COLS = 256
BF16 = jnp.bfloat16
F32 = jnp.float32


def pairs(target):
    index = np.arange(128).reshape(SHAPE)
    return [(int(index[k]), int(index[tuple(target(*k))])) for k in np.ndindex(*SHAPE)]


def along_y(k):
    return pairs(lambda z, h, y, l, c: (z, h, (y - k) % 4, l, c))


def along_z(k):
    return pairs(lambda z, h, y, l, c: ((z - k) % 4, h, y, l, c))


ACROSS_X = pairs(lambda z, h, y, l, c: (z, 1 - h, y, 1 - l, c))
OTHER_CORE = pairs(lambda z, h, y, l, c: (z, h, y, l, 1 - c))
OTHER_CHIP = pairs(lambda z, h, y, l, c: (z, h, y, 1 - l, c))
OTHER_BOTH = pairs(lambda z, h, y, l, c: (z, h, y, 1 - l, 1 - c))


def permute(x, table):
    return lax.ppermute(x, AXES, table)


def packed(factor_a_o, factor_a_down, column):
    def rows(factor):
        own = lax.dynamic_index_in_dim(factor, column, 2, keepdims=False)
        return own.reshape(128, own.shape[-1]).T

    return jnp.concatenate([rows(factor_a_down), rows(factor_a_o)], 0)


def shard_of(dz, dy, h):
    z, xh, y = (lax.axis_index(name) for name in FSDP)
    far = lax.rem(z + (dz + 4), 4)
    side = lax.rem(xh + h, 2)
    return far * 8 + side * 4 + lax.rem(y + (dy + 4), 4)


def shards(half, piece):
    for j, h in np.ndindex(4, 2):
        if half == 0:
            yield shard_of(STEPS[piece], STEPS[j], int(h))
        else:
            yield shard_of(STEPS[j], STEPS[piece], int(h))


def start_of(f, rows, offset):
    return pl.multiple_of(f * rows + offset, 16)


def weights_kernel(bo_ref, bd_ref, wo_ref, wd_ref):
    for b_ref, w_ref in ((bo_ref, wo_ref), (bd_ref, wd_ref)):
        none = jnp.zeros((64, COLS), BF16)
        quarter = jnp.asarray(0.25, F32)
        b = [(b_ref[l].astype(F32) * quarter).astype(BF16) for l in range(2)]
        w_ref[0:64, 0:COLS] = b[0]
        w_ref[0:64, COLS:] = none
        w_ref[64:128, 0:COLS] = none
        w_ref[64:128, COLS:] = b[1]


def deltas(half, a, wo_ref, wd_ref, d_ref):
    if half == 0:
        d_ref[...] = jnp.dot(
            a.reshape(8 * HALF, 128), wd_ref[...], preferred_element_type=F32
        )
    else:
        d_ref[: 8 * TAIL] = jnp.dot(
            a[:, :TAIL].reshape(8 * TAIL, 128), wd_ref[...], preferred_element_type=F32
        )
        d_ref[8 * TAIL :] = jnp.dot(
            a[:, TAIL:].reshape(8 * ATTN, 128), wo_ref[...], preferred_element_type=F32
        )


def parts(half, s, f):
    if half == 0:
        yield 1, start_of(f, DOWN, 0), s * HALF, HALF
    else:
        yield 1, start_of(f, DOWN, HALF), s * TAIL, TAIL
        yield 0, start_of(f, ATTN, 0), 8 * TAIL + s * ATTN, ATTN


def squares_kernel(half, pieces, *refs):
    n = len(pieces)
    a_refs = refs[:n]
    wo_ref, wd_ref, base_o_ref, base_d_ref, out_ref, d_ref = refs[n:]
    acc = {(p, l): jnp.zeros((8, COLS), F32) for p in range(2) for l in range(2)}
    for piece, a_ref in zip(pieces, a_refs):
        deltas(half, a_ref[...], wo_ref, wd_ref, d_ref)
        for s, f in enumerate(shards(half, piece)):
            for p, row, at, rows in parts(half, s, f):
                base_ref = (base_o_ref, base_d_ref)[p]
                for l in range(2):
                    summed = (
                        base_ref[l, pl.ds(row, rows), :].astype(F32)
                        + d_ref[at : at + rows, l * COLS : (l + 1) * COLS]
                    )
                    acc[p, l] += jnp.sum((summed * summed).reshape(rows // 8, 8, COLS), 0)
    for p in range(2):
        for l in range(2):
            out_ref[p, l] = acc[p, l]


def merge_kernel(*refs):
    a_refs = refs[:8]
    (wo_ref, wd_ref, base_o_ref, base_d_ref, square_ref, mag_o_ref, mag_d_ref) = refs[8:15]
    out_o_ref, out_d_ref, buf_o, buf_d, d_ref, sem = refs[15:]
    scale = {}
    for p, mag_ref in enumerate((mag_o_ref, mag_d_ref)):
        for l in range(2):
            scale[p, l] = mag_ref[l : l + 1, :] * lax.rsqrt(square_ref[p, l : l + 1, :] + 1e-06)
    outs = ((buf_o, out_o_ref), (buf_d, out_d_ref))
    for half in range(2):
        for piece in range(4):
            deltas(half, a_refs[half * 4 + piece][...], wo_ref, wd_ref, d_ref)
            for s, f in enumerate(shards(half, piece)):
                for p, row, at, rows in parts(half, s, f):
                    base_ref = (base_o_ref, base_d_ref)[p]
                    buf, out = outs[p]
                    for l in range(2):
                        summed = (
                            base_ref[l, pl.ds(row, rows), :].astype(F32)
                            + d_ref[at : at + rows, l * COLS : (l + 1) * COLS]
                        )
                        buf[l, pl.ds(row, rows), :] = (summed * scale[p, l]).astype(BF16)
                    pltpu.make_async_copy(
                        buf.at[:, pl.ds(row, rows), :], out.at[:, pl.ds(row, rows), :], sem.at[p]
                    ).start()
    for p, (buf, out) in enumerate(outs):
        pltpu.make_async_copy(buf, out, sem.at[p]).wait()


VMEM = pl.BlockSpec(memory_space=pltpu.VMEM)
ANY = pl.BlockSpec(memory_space=pl.ANY)


def call(kernel, outs, n_in, out_specs, scratch=(), cost=None):
    return pl.pallas_call(
        kernel,
        out_shape=outs,
        in_specs=[VMEM] * n_in,
        out_specs=out_specs,
        scratch_shapes=list(scratch),
        cost_estimate=cost,
    )


def local(
    base_o,
    base_down,
    factor_a_o,
    factor_b_o,
    factor_a_down,
    factor_b_down,
    magnitude_o,
    magnitude_down,
):
    column = lax.axis_index(TP)
    own = packed(factor_a_o, factor_a_down, column)
    sent = packed(factor_a_o, factor_a_down, lax.rem(column + 2, 4))
    w_shape = jax.ShapeDtypeStruct((128, 2 * COLS), BF16)
    wo, wd = call(weights_kernel, (w_shape, w_shape), 2, (VMEM, VMEM))(
        jnp.swapaxes(factor_b_o, 1, 2), jnp.swapaxes(factor_b_down, 1, 2)
    )
    got = permute(sent, ACROSS_X)
    first = jnp.stack([own[:HALF], got[:HALF]])
    second = jnp.stack([own[HALF:], got[HALF:]])
    first = jnp.concatenate([first] + [permute(first, along_y(k)) for k in STEPS[1:]])
    second = jnp.concatenate([second] + [permute(second, along_z(k)) for k in STEPS[1:]])
    pieces = [
        [first] + [permute(first, along_z(k)) for k in STEPS[1:]],
        [second] + [permute(second, along_y(k)) for k in STEPS[1:]],
    ]
    partial = []
    for half in range(2):
        for group in ((0,), (1, 2, 3)):
            cost = pl.CostEstimate(
                flops=len(group) * 2 * 1152 * 128 * 512,
                bytes_accessed=len(group) * 2 * 1152 * 512,
                transcendentals=0,
            )
            partial.append(
                call(
                    functools.partial(squares_kernel, half, group),
                    jax.ShapeDtypeStruct((2, 2, 8, COLS), F32),
                    len(group) + 4,
                    VMEM,
                    (pltpu.VMEM((8 * HALF, 2 * COLS), F32),),
                    cost,
                )(*[pieces[half][g] for g in group], wo, wd, base_o, base_down)
            )
    square = jnp.sum(sum(partial), axis=2)
    square = (
        square
        + permute(square, OTHER_CORE)
        + permute(square, OTHER_CHIP)
        + permute(square, OTHER_BOTH)
    )
    return tuple(
        pl.pallas_call(
            merge_kernel,
            out_shape=(
                jax.ShapeDtypeStruct(base_o.shape, BF16),
                jax.ShapeDtypeStruct(base_down.shape, BF16),
            ),
            in_specs=[VMEM] * 15,
            out_specs=(ANY, ANY),
            scratch_shapes=[
                pltpu.VMEM(base_o.shape, BF16),
                pltpu.VMEM(base_down.shape, BF16),
                pltpu.VMEM((8 * HALF, 2 * COLS), F32),
                pltpu.SemaphoreType.DMA((2,)),
            ],
        )(
            *pieces[0],
            *pieces[1],
            wo,
            wd,
            base_o,
            base_down,
            square,
            magnitude_o,
            magnitude_down,
        )
    )


def solution(mesh):
    finer = Mesh(mesh.devices.reshape(SHAPE), AXES)
    in_specs = (
        P(None, TP, FSDP),
        P(None, TP, FSDP),
        P(None, None, None, FSDP),
        P(None, FSDP, None),
        P(None, None, None, FSDP),
        P(None, FSDP, None),
        P(None, FSDP),
        P(None, FSDP),
    )
    out_specs = (P(None, TP, FSDP), P(None, TP, FSDP))
    return jax.shard_map(local, mesh=finer, in_specs=in_specs, out_specs=out_specs, check_vma=False)
```

time: 97.7 us -> 74 us (0.76)
  Pallas kernels: 0 us -> 31.5 us
  blocking collectives: 16.9 us -> 0 us
  matrix products: 13.6 us -> 0 us
  other arithmetic: 13.5 us -> 1.42 us
  local copies, waits for them, and re-layouts: 18 us -> 5.93 us
  waiting for transfers between devices: 11.6 us -> 4.13 us
  starting transfers between devices: 22.6 us -> 29.6 us
    pallas_call x0 -> x6, Pallas kernels: none -> 31.5 us  [the longest x4 21.6 us: local(): call(functools.partial(squares_kernel, half, group), jax.ShapeDtypeStruct...]
    ppermute x0 -> x16, starting transfers between devices: none -> 29.6 us  [permute(): return lax.ppermute(x, AXES, table)]
    all_to_all x3 -> x0, starting transfers between devices: 22.6 us -> none  [copy_for_each(): lax.all_to_all(jnp.broadcast_to(shard[None], (devices, *shard.shape)), ax...]
    psum x2 -> x0, blocking collectives: 16.9 us -> none  [one_axis_at_a_time(): shard = lax.psum(shard, axis)]
    dot_general x2 -> x0, matrix products: 13.6 us -> none  [low_rank(): jnp.einsum('lri,lor->lio', rows_a, factor_b, preferred_element_type=jnp.f...]
    convert_element_type x2 -> x0, other arithmetic: 13.5 us -> none  [finish(): (magnitude[:, None, :] * summed * lax.rsqrt(square + 1e-06)[:, None, :])....]
    all_to_all x3 -> x0, waiting for transfers between devices: 11.6 us -> none  [copy_for_each(): lax.all_to_all(jnp.broadcast_to(shard[None], (devices, *shard.shape)), ax...]
    reshape x2 -> x4, local copies, waits for them, and re-layouts: 6.37 us -> 0.38 us  [rows(): return own.reshape(128, own.shape[-1]).T]
  transfers between devices with their start and end apart: 3 -> 16, of which waited for: 2 -> 3; matrix products, arithmetic and copies ran while one was open for 15% -> 0% of each run, Pallas kernels for 0% -> 24%
where the time goes in v1:
time: 74 us; the launch traced here: 73.7 us
  Pallas kernels  31.5 us (43%)
  starting transfers between devices  29.6 us (40%)
  local copies, waits for them, and re-layouts  5.93 us (8%)
  waiting for transfers between devices  4.13 us (6%)
  other arithmetic  1.42 us (2%)
  between operations  1.04 us (1%)
    ppermute x16, starting transfers between devices, permute(): return lax.ppermute(x, AXES, table)  29.6 us
    pallas_call x4, Pallas kernels, local(): call(functools.partial(squares_kernel, half, group), jax.ShapeDtypeStruct...  21.6 us
    pallas_call x1, Pallas kernels, local(): pl.pallas_call(merge_kernel, out_shape=(jax.ShapeDtypeStruct(base_o.shape...  8.25 us
    ppermute x16, waiting for transfers between devices, permute(): return lax.ppermute(x, AXES, table)  4.13 us
    unnamed x31, local copies, waits for them, and re-layouts  3.07 us
    dynamic_slice x2, local copies, waits for them, and re-layouts, rows(): own = lax.dynamic_index_in_dim(factor, column, 2, keepdims=False)  2.44 us
    pallas_call x1, Pallas kernels, local(): call(weights_kernel, (w_shape, w_shape), 2, (VMEM, VMEM))  1.7 us
  transfers between devices with their start and end apart: 16, of which 3 were waited for; matrix products, arithmetic and copies ran while one was open for 0% of the time, Pallas kernels for 24%

profile of v1, /device:TPU:1, one launch (start us, length us, event | category | flops | bytes accessed | tf_op | source)
XLA Modules:
  0.0 73.7 jit_solution(3262213056868198729)
XLA Ops:
  0.6 1.1 %constant_dynamic-slice_fusion = (bf16[2,64,1,64]{3,2,1,0:T(2,128)(2,1)S(1)}, bf16[2,64,1,64]{3,2,1,0:T(2,128)(2,1)S(1)}) fusion(bf16[2,64,4,64]{3,2,1,0:T(4,128)(2,1)} %param.10, s32[]{:T(128)S(6)} %select_n.10, s32[]{:T(128)S(6)} %select_n.11), kind=kLoop, calls=%fused_computation.20 | loop fusion | bytes 65544 | tf_op jit(solution)/shard_map/jit(dynamic_index_in_dim)/dynamic_slice | solution.py:51
  1.8 0.1 copy.18
  1.9 1.3 %constant_dynamic-slice_fusion.2 = (bf16[2,64,1,224]{3,2,1,0:T(2,128)(2,1)S(1)}, bf16[2,64,1,224]{3,2,1,0:T(2,128)(2,1)S(1)}) fusion(bf16[2,64,4,224]{3,2,1,0:T(4,128)(2,1)} %param.12, s32[]{:T(128)S(6)} %select_n.11, s32[]{:T(128)S(6)} %select_n.10), kind=kLoop, calls=%fused_computation.22 | loop fusion | bytes 229384 | tf_op jit(solution)/shard_map/jit(dynamic_index_in_dim)/dynamic_slice | solution.py:51
  3.2 0.1 copy.15
  3.3 3.4 %collective-permute-start = (bf16[288,128]{1,0:T(8,128)(2,1)S(1)}, bf16[288,128]{1,0:T(8,128)(2,1)S(1)}, u32[]{:S(2)}, u32[]{:S(2)}) collective-permute-start(bf16[288,128]{1,0:T(8,128)(2,1)S(1)} %pad_maximum_fusion), channel_id=1, source_target_pairs={{0,18},{1,19},{2,16},{3,17},{4,22},{5,23},{6,20},{7,21},{8,26},{9,... | collective-permute-start | bytes 221192 | tf_op jit(solution)/shard_map/ppermute | solution.py:46
  6.7 0.1 copy.19
  6.8 0.1 copy.14
  7.0 1.5 %collective-permute-done = bf16[288,128]{1,0:T(8,128)(2,1)S(1)} collective-permute-done((bf16[288,128]{1,0:T(8,128)(2,1)S(1)}, bf16[288,128]{1,0:T(8,128)(2,1)S(1)}, u32[]{:S(2)}, u32[]{:S(2)}) %collective-permute-start) | collective-permute-done | bytes 73760 | tf_op jit(solution)/shard_map/ppermute | solution.py:46
  8.5 3.2 %collective-permute-start.3 = (bf16[2,144,128]{2,1,0:T(8,128)(2,1)S(1)}, bf16[2,144,128]{2,1,0:T(8,128)(2,1)S(1)}, u32[]{:S(2)}, u32[]{:S(2)}) collective-permute-start(bf16[2,144,128]{2,1,0:T(8,128)(2,1)S(1)} %pad_maximum_fusion.1), channel_id=1, source_target_pairs={{0,8},{1,9},{2,10},{3,11},{4,12},{5,13},{6,14},{7,15},{8,0},{9,1},... | collective-permute-start | bytes 221192 | tf_op jit(solution)/shard_map/ppermute | solution.py:46
  11.7 0.8 %collective-permute-start.2 = (bf16[2,144,128]{2,1,0:T(8,128)(2,1)S(1)}, bf16[2,144,128]{2,1,0:T(8,128)(2,1)S(1)}, u32[]{:S(2)}, u32[]{:S(2)}) collective-permute-start(bf16[2,144,128]{2,1,0:T(8,128)(2,1)S(1)} %pad_maximum_fusion.1), channel_id=1, source_target_pairs={{0,12},{1,13},{2,14},{3,15},{4,0},{5,1},{6,2},{7,3},{8,4},{9,5},{1... | collective-permute-start | bytes 221192 | tf_op jit(solution)/shard_map/ppermute | solution.py:46
  12.4 0.7 collective-permute-start.1
  13.1 3.7 %collective-permute-start.9 = (bf16[2,144,128]{2,1,0:T(8,128)(2,1)S(1)}, bf16[2,144,128]{2,1,0:T(8,128)(2,1)S(1)}, u32[]{:S(2)}, u32[]{:S(2)}) collective-permute-start(bf16[2,144,128]{2,1,0:T(8,128)(2,1)S(1)} %pad_maximum_fusion.2), channel_id=1, source_target_pairs={{0,64},{1,65},{2,66},{3,67},{4,68},{5,69},{6,70},{7,71},{8,72},{9,... | collective-permute-start | bytes 221192 | tf_op jit(solution)/shard_map/ppermute | solution.py:46
  16.8 0.4 collective-permute-start.8
  17.3 0.0 collective-permute-done.1
  17.3 1.4 %collective-permute-start.7 = (bf16[2,144,128]{2,1,0:T(8,128)(2,1)S(1)}, bf16[2,144,128]{2,1,0:T(8,128)(2,1)S(1)}, u32[]{:S(2)}, u32[]{:S(2)}) collective-permute-start(bf16[2,144,128]{2,1,0:T(8,128)(2,1)S(1)} %pad_maximum_fusion.2), channel_id=1, source_target_pairs={{0,32},{1,33},{2,34},{3,35},{4,36},{5,37},{6,38},{7,39},{8,40},{9,... | collective-permute-start | bytes 221192 | tf_op jit(solution)/shard_map/ppermute | solution.py:46
  18.7 0.0 collective-permute-done.2
  18.8 0.0 collective-permute-done.3
  18.8 0.0 copy-start.1
  18.8 3.4 %collective-permute-start.6 = (bf16[8,144,128]{2,1,0:T(8,128)(2,1)S(1)}, bf16[8,144,128]{2,1,0:T(8,128)(2,1)S(1)}, u32[]{:S(2)}, u32[]{:S(2)}) collective-permute-start(bf16[8,144,128]{2,1,0:T(8,128)(2,1)S(1)} %constant_dynamic-update-slice_fusion.refs_0_), channel_id=1, source_target_pairs={{0,64},{1,65},{2,66},{3,67},{4,68},{5,69},{6,70},{7,71},{8,72},{9,... | collective-permute-start | bytes 884744 | tf_op jit(solution)/shard_map/ppermute | solution.py:46
  22.2 0.7 collective-permute-start.5
  22.9 0.0 collective-permute-done.7
  22.9 0.7 %collective-permute-start.4 = (bf16[8,144,128]{2,1,0:T(8,128)(2,1)S(1)}, bf16[8,144,128]{2,1,0:T(8,128)(2,1)S(1)}, u32[]{:S(2)}, u32[]{:S(2)}) collective-permute-start(bf16[8,144,128]{2,1,0:T(8,128)(2,1)S(1)} %constant_dynamic-update-slice_fusion.refs_0_), channel_id=1, source_target_pairs={{0,32},{1,33},{2,34},{3,35},{4,36},{5,37},{6,38},{7,39},{8,40},{9,... | collective-permute-start | bytes 884744 | tf_op jit(solution)/shard_map/ppermute | solution.py:46
  23.7 0.0 collective-permute-done.8
  23.7 0.0 collective-permute-done.9
  23.7 0.0 copy-start
  23.7 0.2 collective-permute-start.12
  23.9 1.9 %collective-permute-start.11 = (bf16[8,144,128]{2,1,0:T(8,128)(2,1)S(1)}, bf16[8,144,128]{2,1,0:T(8,128)(2,1)S(1)}, u32[]{:S(2)}, u32[]{:S(2)}) collective-permute-start(bf16[8,144,128]{2,1,0:T(8,128)(2,1)S(1)} %constant_dynamic-update-slice_fusion.5.refs_0_.refs_4_), channel_id=1, source_target_pairs={{0,12},{1,13},{2,14},{3,15},{4,0},{5,1},{6,2},{7,3},{8,4},{9,5},{1... | collective-permute-start | bytes 884744 | tf_op jit(solution)/shard_map/ppermute | solution.py:46
  25.8 1.4 %collective-permute-done.6.refs_2_.refs_3_ = bf16[8,144,128]{2,1,0:T(8,128)(2,1)S(1)} collective-permute-done((bf16[8,144,128]{2,1,0:T(8,128)(2,1)S(1)}, bf16[8,144,128]{2,1,0:T(8,128)(2,1)S(1)}, u32[]{:S(2)}, u32[]{:S(2)}) %collective-permute-start.6) | collective-permute-done | bytes 294944 | tf_op jit(solution)/shard_map/ppermute | solution.py:46
  27.1 0.0 copy-start.2
  27.1 0.0 collective-permute-start.10
  27.1 1.7 %shard_map.95 = (bf16[128,512]{1,0:T(8,128)(2,1)}, bf16[128,512]{1,0:T(8,128)(2,1)}) custom-call(bf16[2,64,256]{2,1,0:T(8,128)(2,1)} %bitcast.34, bf16[2,64,256]{2,1,0:T(8,128)(2,1)} %bitcast.35), custom_call_target="tpu_custom_call" | custom-call | tf_op jit(solution)/shard_map/pallas_call | solution.py:188
  28.8 0.0 copy-done
  28.8 5.0 %shard_map.98 = f32[2,2,8,256]{3,2,1,0:T(8,128)} custom-call(bf16[8,144,128]{2,1,0:T(8,128)(2,1)} %copy-done, bf16[128,512]{1,0:T(8,128)(2,1)} %get-tuple-element.4.refs_1_.refs_3_.refs_8_, bf16[128,512]{1,0:T(8,128)(2,1)} %get-tuple-element.5.refs_2_.refs_4_.refs_9_, bf16[2,2048,256]{2,1,0:T(8,128)(2,1)} %refs_10_.1, bf16[2,7168,256]{2,1,0:T(8,128)(2,1)} %refs_11_.1), custom_call_target="tpu_custom_call" | custom-call | flops 150994944 | bytes 1179648 | tf_op jit(solution)/shard_map/pallas_call | solution.py:209
  33.8 0.0 copy-done.1
  33.8 5.0 %shard_map.96 = f32[2,2,8,256]{3,2,1,0:T(8,128)} custom-call(bf16[8,144,128]{2,1,0:T(8,128)(2,1)} %copy-done.1, bf16[128,512]{1,0:T(8,128)(2,1)} %get-tuple-element.4.refs_1_.refs_3_.refs_8_, bf16[128,512]{1,0:T(8,128)(2,1)} %get-tuple-element.5.refs_2_.refs_4_.refs_9_, bf16[2,2048,256]{2,1,0:T(8,128)(2,1)} %refs_10_.1, bf16[2,7168,256]{2,1,0:T(8,128)(2,1)} %refs_11_.1), custom_call_target="tpu_custom_call" | custom-call | flops 150994944 | bytes 1179648 | tf_op jit(solution)/shard_map/pallas_call | solution.py:209
  38.8 0.0 copy-done.2
  38.8 0.0 collective-permute-done.5.refs_1_.refs_2_
  38.8 0.0 copy-start.3
  38.8 0.0 collective-permute-done.4.refs_0_.refs_1_
  38.8 0.7 copy-done.3
  39.5 0.0 copy-start.4
  39.5 0.7 copy-done.4
  40.2 5.8 %shard_map.97 = f32[2,2,8,256]{3,2,1,0:T(8,128)} custom-call(bf16[8,144,128]{2,1,0:T(8,128)(2,1)} %copy-done.4, bf16[8,144,128]{2,1,0:T(8,128)(2,1)} %copy-done.3, bf16[8,144,128]{2,1,0:T(8,128)(2,1)} %copy-done.2, bf16[128,512]{1,0:T(8,128)(2,1)} %get-tuple-element.4.refs_1_.refs_3_.refs_8_, bf16[128,512]{1,0:T(8,128)(2,1)} %get-tuple-element.5.refs_2_.refs_4_.refs_9_, ...), custom_call_target="tpu_custom_call" | custom-call | flops 452984832 | bytes 3538944 | tf_op jit(solution)/shard_map/pallas_call | solution.py:209
  46.0 0.0 collective-permute-done.12.refs_2_.refs_7_
  46.0 0.0 copy-start.5
  46.1 0.0 collective-permute-done.11.refs_1_.refs_6_
  46.1 0.0 copy-start.6
  46.1 0.0 collective-permute-done.10.refs_0_.refs_5_
  46.1 0.7 copy-done.5
  46.8 0.1 copy-done.6
  46.9 0.7 copy-done.7
  47.6 5.8 %shard_map.99 = f32[2,2,8,256]{3,2,1,0:T(8,128)} custom-call(bf16[8,144,128]{2,1,0:T(8,128)(2,1)} %copy-done.7, bf16[8,144,128]{2,1,0:T(8,128)(2,1)} %copy-done.6, bf16[8,144,128]{2,1,0:T(8,128)(2,1)} %copy-done.5, bf16[128,512]{1,0:T(8,128)(2,1)} %get-tuple-element.4.refs_1_.refs_3_.refs_8_, bf16[128,512]{1,0:T(8,128)(2,1)} %get-tuple-element.5.refs_2_.refs_4_.refs_9_, ...), custom_call_target="tpu_custom_call" | custom-call | flops 452984832 | bytes 3538944 | tf_op jit(solution)/shard_map/pallas_call | solution.py:209
  53.4 0.0 copy-done.8
  53.4 0.0 copy-done.9
  53.4 0.0 copy-done.10
  53.4 0.8 %add_reduce_fusion = f32[2,2,256]{2,1,0:T(2,128)S(1)} fusion(f32[2,2,8,256]{3,2,1,0:T(8,128)} %shard_map.99, f32[2,2,8,256]{3,2,1,0:T(8,128)S(1)} %copy-done.8, f32[2,2,8,256]{3,2,1,0:T(8,128)S(1)} %copy-done.9, f32[2,2,8,256]{3,2,1,0:T(8,128)S(1)} %copy-done.10), kind=kLoop, calls=%fused_computation.8 | loop fusion | flops 31744 | bytes 135168 | tf_op jit(solution)/shard_map/reduce_sum | solution.py:218
  54.2 7.7 %collective-permute-start.15 = (f32[2,2,256]{2,1,0:T(2,128)S(1)}, f32[2,2,256]{2,1,0:T(2,128)S(1)}, u32[]{:S(2)}, u32[]{:S(2)}) collective-permute-start(f32[2,2,256]{2,1,0:T(2,128)S(1)} %add_reduce_fusion), channel_id=1, source_target_pairs={{0,3},{1,2},{2,1},{3,0},{4,7},{5,6},{6,5},{7,4},{8,11},{9,10},{10,... | collective-permute-start | bytes 12296 | tf_op jit(solution)/shard_map/ppermute | solution.py:46
  61.9 1.5 %collective-permute-start.14 = (f32[2,2,256]{2,1,0:T(2,128)S(1)}, f32[2,2,256]{2,1,0:T(2,128)S(1)}, u32[]{:S(2)}, u32[]{:S(2)}) collective-permute-start(f32[2,2,256]{2,1,0:T(2,128)S(1)} %add_reduce_fusion), channel_id=1, source_target_pairs={{0,2},{1,3},{2,0},{3,1},{4,6},{5,7},{6,4},{7,5},{8,10},{9,11},{10,... | collective-permute-start | bytes 12296 | tf_op jit(solution)/shard_map/ppermute | solution.py:46
  63.4 0.0 collective-permute-start.13
  63.4 0.0 collective-permute-done.15
  63.4 1.3 %collective-permute-done.14 = f32[2,2,256]{2,1,0:T(2,128)S(1)} collective-permute-done((f32[2,2,256]{2,1,0:T(2,128)S(1)}, f32[2,2,256]{2,1,0:T(2,128)S(1)}, u32[]{:S(2)}, u32[]{:S(2)}) %collective-permute-start.14) | collective-permute-done | bytes 4128 | tf_op jit(solution)/shard_map/ppermute | solution.py:46
  64.6 0.0 collective-permute-done.13
  64.7 0.6 add_add_fusion.refs_12_
  65.2 8.3 %shard_map.100 = (bf16[2,2048,256]{2,1,0:T(8,128)(2,1)}, bf16[2,7168,256]{2,1,0:T(8,128)(2,1)}) custom-call(bf16[8,144,128]{2,1,0:T(8,128)(2,1)} %copy-done.1, bf16[8,144,128]{2,1,0:T(8,128)(2,1)} %copy-done.4, bf16[8,144,128]{2,1,0:T(8,128)(2,1)} %copy-done.3, bf16[8,144,128]{2,1,0:T(8,128)(2,1)} %copy-done.2, bf16[8,144,128]{2,1,0:T(8,128)(2,1)} %copy-done, ...), custom_call_target="tpu_custom_call" | custom-call | tf_op jit(solution)/shard_map/pallas_call | solution.py:226
  (21 shorter events, 0.2 us)
Async XLA Ops:
  3.3 5.1 %collective-permute-start = (bf16[288,128]{1,0:T(8,128)(2,1)S(1)}, bf16[288,128]{1,0:T(8,128)(2,1)S(1)}, u32[]{:S(2)}, u32[]{:S(2)}) collective-permute-start(bf16[288,128]{1,0:T(8,128)(2,1)S(1)} %pad_maximum_fusion), channel_id=1, source_target_pairs={{0,18},{1,19},{2,16},{3,17},{4,22},{5,23},{6,20},{7,21},{8,26},{9,... | collective-permute-start | bytes 221192 | tf_op jit(solution)/shard_map/ppermute | solution.py:46
  8.5 10.3 %collective-permute-start.3 = (bf16[2,144,128]{2,1,0:T(8,128)(2,1)S(1)}, bf16[2,144,128]{2,1,0:T(8,128)(2,1)S(1)}, u32[]{:S(2)}, u32[]{:S(2)}) collective-permute-start(bf16[2,144,128]{2,1,0:T(8,128)(2,1)S(1)} %pad_maximum_fusion.1), channel_id=1, source_target_pairs={{0,8},{1,9},{2,10},{3,11},{4,12},{5,13},{6,14},{7,15},{8,0},{9,1},... | collective-permute-start | bytes 221192 | tf_op jit(solution)/shard_map/ppermute | solution.py:46
  11.7 7.1 %collective-permute-start.2 = (bf16[2,144,128]{2,1,0:T(8,128)(2,1)S(1)}, bf16[2,144,128]{2,1,0:T(8,128)(2,1)S(1)}, u32[]{:S(2)}, u32[]{:S(2)}) collective-permute-start(bf16[2,144,128]{2,1,0:T(8,128)(2,1)S(1)} %pad_maximum_fusion.1), channel_id=1, source_target_pairs={{0,12},{1,13},{2,14},{3,15},{4,0},{5,1},{6,2},{7,3},{8,4},{9,5},{1... | collective-permute-start | bytes 221192 | tf_op jit(solution)/shard_map/ppermute | solution.py:46
  12.4 4.8 %collective-permute-start.1 = (bf16[2,144,128]{2,1,0:T(8,128)(2,1)S(1)}, bf16[2,144,128]{2,1,0:T(8,128)(2,1)S(1)}, u32[]{:S(2)}, u32[]{:S(2)}) collective-permute-start(bf16[2,144,128]{2,1,0:T(8,128)(2,1)S(1)} %pad_maximum_fusion.1), channel_id=1, source_target_pairs={{0,4},{1,5},{2,6},{3,7},{4,8},{5,9},{6,10},{7,11},{8,12},{9,13},{1... | collective-permute-start | bytes 221192 | tf_op jit(solution)/shard_map/ppermute | solution.py:46
  13.1 10.6 %collective-permute-start.9 = (bf16[2,144,128]{2,1,0:T(8,128)(2,1)S(1)}, bf16[2,144,128]{2,1,0:T(8,128)(2,1)S(1)}, u32[]{:S(2)}, u32[]{:S(2)}) collective-permute-start(bf16[2,144,128]{2,1,0:T(8,128)(2,1)S(1)} %pad_maximum_fusion.2), channel_id=1, source_target_pairs={{0,64},{1,65},{2,66},{3,67},{4,68},{5,69},{6,70},{7,71},{8,72},{9,... | collective-permute-start | bytes 221192 | tf_op jit(solution)/shard_map/ppermute | solution.py:46
  16.8 6.9 %collective-permute-start.8 = (bf16[2,144,128]{2,1,0:T(8,128)(2,1)S(1)}, bf16[2,144,128]{2,1,0:T(8,128)(2,1)S(1)}, u32[]{:S(2)}, u32[]{:S(2)}) collective-permute-start(bf16[2,144,128]{2,1,0:T(8,128)(2,1)S(1)} %pad_maximum_fusion.2), channel_id=1, source_target_pairs={{0,96},{1,97},{2,98},{3,99},{4,100},{5,101},{6,102},{7,103},{8,104... | collective-permute-start | bytes 221192 | tf_op jit(solution)/shard_map/ppermute | solution.py:46
  17.3 5.6 %collective-permute-start.7 = (bf16[2,144,128]{2,1,0:T(8,128)(2,1)S(1)}, bf16[2,144,128]{2,1,0:T(8,128)(2,1)S(1)}, u32[]{:S(2)}, u32[]{:S(2)}) collective-permute-start(bf16[2,144,128]{2,1,0:T(8,128)(2,1)S(1)} %pad_maximum_fusion.2), channel_id=1, source_target_pairs={{0,32},{1,33},{2,34},{3,35},{4,36},{5,37},{6,38},{7,39},{8,40},{9,... | collective-permute-start | bytes 221192 | tf_op jit(solution)/shard_map/ppermute | solution.py:46
  18.8 15.0 %copy-start.1 = (bf16[8,144,128]{2,1,0:T(8,128)(2,1)}, bf16[8,144,128]{2,1,0:T(8,128)(2,1)S(1)}, u32[]{:S(2)}) copy-start(bf16[8,144,128]{2,1,0:T(8,128)(2,1)S(1)} %constant_dynamic-update-slice_fusion.refs_0_) | copy-start | bytes 884740
  18.8 8.3 %collective-permute-start.6 = (bf16[8,144,128]{2,1,0:T(8,128)(2,1)S(1)}, bf16[8,144,128]{2,1,0:T(8,128)(2,1)S(1)}, u32[]{:S(2)}, u32[]{:S(2)}) collective-permute-start(bf16[8,144,128]{2,1,0:T(8,128)(2,1)S(1)} %constant_dynamic-update-slice_fusion.refs_0_), channel_id=1, source_target_pairs={{0,64},{1,65},{2,66},{3,67},{4,68},{5,69},{6,70},{7,71},{8,72},{9,... | collective-permute-start | bytes 884744 | tf_op jit(solution)/shard_map/ppermute | solution.py:46
  22.2 16.6 %collective-permute-start.5 = (bf16[8,144,128]{2,1,0:T(8,128)(2,1)S(1)}, bf16[8,144,128]{2,1,0:T(8,128)(2,1)S(1)}, u32[]{:S(2)}, u32[]{:S(2)}) collective-permute-start(bf16[8,144,128]{2,1,0:T(8,128)(2,1)S(1)} %constant_dynamic-update-slice_fusion.refs_0_), channel_id=1, source_target_pairs={{0,96},{1,97},{2,98},{3,99},{4,100},{5,101},{6,102},{7,103},{8,104... | collective-permute-start | bytes 884744 | tf_op jit(solution)/shard_map/ppermute | solution.py:46
  22.9 15.9 %collective-permute-start.4 = (bf16[8,144,128]{2,1,0:T(8,128)(2,1)S(1)}, bf16[8,144,128]{2,1,0:T(8,128)(2,1)S(1)}, u32[]{:S(2)}, u32[]{:S(2)}) collective-permute-start(bf16[8,144,128]{2,1,0:T(8,128)(2,1)S(1)} %constant_dynamic-update-slice_fusion.refs_0_), channel_id=1, source_target_pairs={{0,32},{1,33},{2,34},{3,35},{4,36},{5,37},{6,38},{7,39},{8,40},{9,... | collective-permute-start | bytes 884744 | tf_op jit(solution)/shard_map/ppermute | solution.py:46
  23.7 5.1 %copy-start = (bf16[8,144,128]{2,1,0:T(8,128)(2,1)}, bf16[8,144,128]{2,1,0:T(8,128)(2,1)S(1)}, u32[]{:S(2)}) copy-start(bf16[8,144,128]{2,1,0:T(8,128)(2,1)S(1)} %constant_dynamic-update-slice_fusion.5.refs_0_.refs_4_) | copy-start | bytes 884740
  23.7 22.3 %collective-permute-start.12 = (bf16[8,144,128]{2,1,0:T(8,128)(2,1)S(1)}, bf16[8,144,128]{2,1,0:T(8,128)(2,1)S(1)}, u32[]{:S(2)}, u32[]{:S(2)}) collective-permute-start(bf16[8,144,128]{2,1,0:T(8,128)(2,1)S(1)} %constant_dynamic-update-slice_fusion.5.refs_0_.refs_4_), channel_id=1, source_target_pairs={{0,8},{1,9},{2,10},{3,11},{4,12},{5,13},{6,14},{7,15},{8,0},{9,1},... | collective-permute-start | bytes 884744 | tf_op jit(solution)/shard_map/ppermute | solution.py:46
  23.9 22.2 %collective-permute-start.11 = (bf16[8,144,128]{2,1,0:T(8,128)(2,1)S(1)}, bf16[8,144,128]{2,1,0:T(8,128)(2,1)S(1)}, u32[]{:S(2)}, u32[]{:S(2)}) collective-permute-start(bf16[8,144,128]{2,1,0:T(8,128)(2,1)S(1)} %constant_dynamic-update-slice_fusion.5.refs_0_.refs_4_), channel_id=1, source_target_pairs={{0,12},{1,13},{2,14},{3,15},{4,0},{5,1},{6,2},{7,3},{8,4},{9,5},{1... | collective-permute-start | bytes 884744 | tf_op jit(solution)/shard_map/ppermute | solution.py:46
  27.1 11.7 %copy-start.2 = (bf16[8,144,128]{2,1,0:T(8,128)(2,1)}, bf16[8,144,128]{2,1,0:T(8,128)(2,1)S(1)}, u32[]{:S(2)}) copy-start(bf16[8,144,128]{2,1,0:T(8,128)(2,1)S(1)} %collective-permute-done.6.refs_2_.refs_3_) | copy-start | bytes 884740
  27.1 19.0 %collective-permute-start.10 = (bf16[8,144,128]{2,1,0:T(8,128)(2,1)S(1)}, bf16[8,144,128]{2,1,0:T(8,128)(2,1)S(1)}, u32[]{:S(2)}, u32[]{:S(2)}) collective-permute-start(bf16[8,144,128]{2,1,0:T(8,128)(2,1)S(1)} %constant_dynamic-update-slice_fusion.5.refs_0_.refs_4_), channel_id=1, source_target_pairs={{0,4},{1,5},{2,6},{3,7},{4,8},{5,9},{6,10},{7,11},{8,12},{9,13},{1... | collective-permute-start | bytes 884744 | tf_op jit(solution)/shard_map/ppermute | solution.py:46
  38.8 0.7 copy-start.3
  39.5 0.7 copy-start.4
  46.0 7.4 %copy-start.8 = (f32[2,2,8,256]{3,2,1,0:T(8,128)S(1)}, f32[2,2,8,256]{3,2,1,0:T(8,128)}, u32[]{:S(2)}) copy-start(f32[2,2,8,256]{3,2,1,0:T(8,128)} %shard_map.98) | copy-start | bytes 98308
  46.0 7.4 %copy-start.9 = (f32[2,2,8,256]{3,2,1,0:T(8,128)S(1)}, f32[2,2,8,256]{3,2,1,0:T(8,128)}, u32[]{:S(2)}) copy-start(f32[2,2,8,256]{3,2,1,0:T(8,128)} %shard_map.96) | copy-start | bytes 98308
  46.0 7.4 %copy-start.10 = (f32[2,2,8,256]{3,2,1,0:T(8,128)S(1)}, f32[2,2,8,256]{3,2,1,0:T(8,128)}, u32[]{:S(2)}) copy-start(f32[2,2,8,256]{3,2,1,0:T(8,128)} %shard_map.97) | copy-start | bytes 98308
  46.0 0.7 copy-start.5
  46.1 0.8 %copy-start.6 = (bf16[8,144,128]{2,1,0:T(8,128)(2,1)}, bf16[8,144,128]{2,1,0:T(8,128)(2,1)S(1)}, u32[]{:S(2)}) copy-start(bf16[8,144,128]{2,1,0:T(8,128)(2,1)S(1)} %collective-permute-done.11.refs_1_.refs_6_) | copy-start | bytes 884740
  46.9 0.7 copy-start.7
  54.2 9.2 %collective-permute-start.15 = (f32[2,2,256]{2,1,0:T(2,128)S(1)}, f32[2,2,256]{2,1,0:T(2,128)S(1)}, u32[]{:S(2)}, u32[]{:S(2)}) collective-permute-start(f32[2,2,256]{2,1,0:T(2,128)S(1)} %add_reduce_fusion), channel_id=1, source_target_pairs={{0,3},{1,2},{2,1},{3,0},{4,7},{5,6},{6,5},{7,4},{8,11},{9,10},{10,... | collective-permute-start | bytes 12296 | tf_op jit(solution)/shard_map/ppermute | solution.py:46
  61.9 2.8 %collective-permute-start.14 = (f32[2,2,256]{2,1,0:T(2,128)S(1)}, f32[2,2,256]{2,1,0:T(2,128)S(1)}, u32[]{:S(2)}, u32[]{:S(2)}) collective-permute-start(f32[2,2,256]{2,1,0:T(2,128)S(1)} %add_reduce_fusion), channel_id=1, source_target_pairs={{0,2},{1,3},{2,0},{3,1},{4,6},{5,7},{6,4},{7,5},{8,10},{9,11},{10,... | collective-permute-start | bytes 12296 | tf_op jit(solution)/shard_map/ppermute | solution.py:46
  63.4 1.3 %collective-permute-start.13 = (f32[2,2,256]{2,1,0:T(2,128)S(1)}, f32[2,2,256]{2,1,0:T(2,128)S(1)}, u32[]{:S(2)}, u32[]{:S(2)}) collective-permute-start(f32[2,2,256]{2,1,0:T(2,128)S(1)} %add_reduce_fusion), channel_id=1, source_target_pairs={{0,1},{1,0},{2,3},{3,2},{4,5},{5,4},{6,7},{7,6},{8,9},{9,8},{10,11... | collective-permute-start | bytes 12296 | tf_op jit(solution)/shard_map/ppermute | solution.py:46
